TPU v7x, 32 devices: a whole 2x2x4 slice. The times are simulated.
32 devices in a mesh: rep: 4 (over y, core), shard: 8 (over z, x).
Axes of the slice: x: 2, y: 2, z: 4, core: 2. Of those that a mesh axis runs over, the one named last changes fastest.
Arguments:
- delta: bfloat16 [4, 512, 6144], P('rep', 'shard'), may hold values from -11 to 11
- counts: int32 [4], replicated, may hold values from 1000 to 7999
- params: bfloat16 [512, 6144], P('shard'), may hold values from -0.078125 to 0.078125
- momentum: float32 [512, 6144], P('shard', 'rep'), may hold values from -4 to 4
Outputs:
- new_params: bfloat16 [512, 6144], P('shard')
- new_momentum: float32 [512, 6144], P('shard', 'rep')
- update_rms: float32 [], replicated
- mean_variance: float32 [], replicated
All inputs are finite; a program needn't handle non-finite values.
Results may differ from a plain program's by a relative error of at most 0.0004.
Values may be sent and summed in bfloat16 or wider, within the bound.
A program may use at most 64 MiB of HBM per device.

v0:
```python
import functools

import jax
import jax.numpy as jnp
from jax import lax
from jax.experimental import pallas as pl
from jax.experimental.pallas import tpu as pltpu
from jax.sharding import PartitionSpec as P

clip_rms = 0.2
beta_outer = 0.9
outer_rate = 0.7
epsilon = 1e-06

MESH = pl.DeviceIdType.MESH
STEP_ROWS = 32
STEP_COLS = 256
UNROLL_MOST = 64


def kernel(
    n_rep, n_shard, element_count,
    delta_ref, counts_ref, params_ref, momentum_ref,
    new_params_ref, new_momentum_ref, rms_ref, mean_var_ref,
    staged, arrived, mean_buf, var_buf, own_params, own_momentum, sums,
    stage_sem, local_sem, send_sem, recv_sem, sum_send_sem, sum_recv_sem, out_send_sem, out_recv_sem, round_sem,
):
    rep = lax.axis_index("rep")
    shard = lax.axis_index("shard")
    n_all = n_rep * n_shard
    me = rep * n_shard + shard
    rows, width = own_momentum.shape
    n_steps = rows // STEP_ROWS

    def column_block(index):
        return pl.ds(pl.multiple_of(index * width, 128), width)

    def row_block(step):
        return pl.ds(step * STEP_ROWS, STEP_ROWS)

    def stage(step):
        return pltpu.make_async_copy(
            delta_ref.at[0, row_block(step)], staged.at[row_block(step)], stage_sem.at[step]
        )

    def device_at(offset):
        other = lax.rem(me + offset, n_all)
        return (other // n_shard, lax.rem(other, n_shard))

    barrier = pltpu.get_barrier_semaphore()

    def along_shard(offset):
        return (rep, lax.rem(shard + offset, n_shard))

    def across_rep(hop):
        return (lax.rem(rep + hop, n_rep), shard)

    beside = sorted({1 % n_shard, (n_shard - 1) % n_shard} - {0})
    greeted = [across_rep(hop) for hop in range(1, n_rep)] + [along_shard(offset) for offset in beside]
    for device in greeted:
        pl.semaphore_signal(barrier, inc=1, device_id=device, device_id_type=MESH)

    for step in range(n_steps):
        stage(step).start()
    load_params = pltpu.make_async_copy(params_ref.at[:, column_block(rep)], own_params, local_sem.at[0])
    load_momentum = pltpu.make_async_copy(momentum_ref, own_momentum, local_sem.at[1])

    pl.semaphore_wait(barrier, len(greeted))

    def exchange(step, hop):
        peer = lax.rem(rep + hop, n_rep)
        return pltpu.make_async_remote_copy(
            src_ref=staged.at[row_block(step), column_block(peer)],
            dst_ref=arrived.at[hop - 1, row_block(step)],
            send_sem=send_sem.at[step, hop - 1],
            recv_sem=recv_sem.at[step, hop - 1],
            device_id=(peer, shard),
            device_id_type=MESH,
        )

    for step in range(n_steps):
        stage(step).wait()
        for hop in range(1, n_rep):
            exchange(step, hop).start()

    load_params.start()
    load_momentum.start()

    known = 1
    level = 0
    while known < n_shard // 2:
        for offset in (known, n_shard - known):
            pl.semaphore_signal(
                round_sem.at[level], inc=1, device_id=along_shard(offset), device_id_type=MESH
            )
        pl.semaphore_wait(round_sem.at[level], 2)
        known, level = 2 * known, level + 1
    for hop in range(1, n_rep):
        pl.semaphore_signal(round_sem.at[level], inc=1, device_id=across_rep(hop), device_id_type=MESH)
    pl.semaphore_wait(round_sem.at[level], n_rep - 1)

    tile = (8, 128)
    total = counts_ref[0]
    for index in range(1, n_rep):
        total = total + counts_ref[index]
    total_tokens = jnp.full(tile, total.astype(jnp.float32))

    def weight_of(index):
        return (jnp.full(tile, counts_ref[index].astype(jnp.float32)) / total_tokens)[0:1, 0:1]

    weights = [weight_of(lax.rem(rep + n_rep - hop, n_rep)) for hop in range(n_rep)]

    square_sum = jnp.zeros(tile, jnp.float32)
    var_sum = jnp.zeros(tile, jnp.float32)
    for step in range(n_steps):
        for hop in range(1, n_rep):
            exchange(step, hop).wait_recv()

        def moments(index, carry):
            square_sum, var_sum = carry
            start = pl.multiple_of(index * STEP_COLS, 128)
            columns = pl.ds(start, STEP_COLS)
            own_columns = pl.ds(pl.multiple_of(rep * width + start, 128), STEP_COLS)
            values = [staged[row_block(step), own_columns].astype(jnp.float32)]
            for hop in range(1, n_rep):
                values.append(arrived[hop - 1, row_block(step), columns].astype(jnp.float32))
            mean = weights[0] * values[0]
            for weight, value in zip(weights[1:], values[1:]):
                mean = mean + weight * value
            variance = jnp.zeros_like(mean)
            for weight, value in zip(weights, values):
                centered = value - mean
                variance = variance + weight * (centered * centered)
            mean_buf[row_block(step), columns] = mean
            var_buf[row_block(step), columns] = variance

            def fold(array):
                out = jnp.zeros(tile, jnp.float32)
                for top in range(0, STEP_ROWS, 8):
                    for left in range(0, STEP_COLS, 128):
                        out = out + array[top:top + 8, left:left + 128]
                return out

            return square_sum + fold(mean * mean), var_sum + fold(variance)

        square_sum, var_sum = lax.fori_loop(0, width // STEP_COLS, moments, (square_sum, var_sum), unroll=True)

    sums[me, 0:1, :] = jnp.sum(square_sum, axis=0, keepdims=True)
    sums[me, 1:2, :] = jnp.sum(var_sum, axis=0, keepdims=True)

    def send_sums(device):
        pltpu.make_async_remote_copy(
            src_ref=sums.at[me],
            dst_ref=sums.at[me],
            send_sem=sum_send_sem,
            recv_sem=sum_recv_sem,
            device_id=device,
            device_id_type=MESH,
        ).start()

    if n_all <= UNROLL_MOST:
        offsets = [(hop, offset) for offset in range(n_shard) for hop in range(n_rep) if hop or offset]
        offsets.sort(key=lambda at: -min(at[1], n_shard - at[1]) - min(at[0], n_rep - at[0]))
        for hop, offset in offsets:
            send_sums((across_rep(hop)[0], along_shard(offset)[1]))
    else:

        @pl.loop(1, n_all)
        def _(offset):
            send_sums(device_at(offset))

    load_params.wait()
    load_momentum.wait()
    others = sums.at[pl.ds(0, n_all - 1)]
    pltpu.make_async_copy(others, others, sum_recv_sem).wait()

    totals = jnp.sum(sums[...], axis=0)
    totals = jnp.sum(totals, axis=1, keepdims=True)
    rms = jnp.sqrt(totals[0:1] / element_count)
    mean_var = totals[1:2] / element_count
    clip_factor = clip_rms / jnp.maximum(rms, clip_rms)
    inverse = 1.0 / (mean_var + epsilon)

    partner = rep + 1 - 2 * lax.rem(rep, 2)
    n_pairs = n_rep // 2

    def send_block(step, owner, target, slot):
        block = new_params_ref.at[row_block(step), column_block(owner)]
        return pltpu.make_async_remote_copy(
            src_ref=block,
            dst_ref=block,
            send_sem=out_send_sem.at[step, slot],
            recv_sem=out_recv_sem.at[step, slot],
            device_id=(target, shard),
            device_id_type=MESH,
        )

    def arriving(step, owner, slot):
        block = new_params_ref.at[row_block(step), column_block(owner)]
        return pltpu.make_async_copy(block, block, out_recv_sem.at[step, slot])

    def to_pair(step, pair):
        return send_block(step, rep, lax.rem(rep + 2 * pair, n_rep), pair - 1)

    def from_pair(step, pair):
        return arriving(step, lax.rem(rep + n_rep - 2 * pair, n_rep), pair - 1)

    def to_partner(step, pair):
        return send_block(step, lax.rem(rep + n_rep - 2 * pair, n_rep), partner, n_pairs - 1 + pair)

    def from_partner(step, pair):
        return arriving(step, lax.rem(partner + n_rep - 2 * pair, n_rep), n_pairs - 1 + pair)

    for step in range(n_steps):

        @pl.loop(0, width // STEP_COLS, unroll=True)
        def _(index):
            start = pl.multiple_of(index * STEP_COLS, 128)
            columns = pl.ds(start, STEP_COLS)
            own_columns = pl.ds(pl.multiple_of(rep * width + start, 128), STEP_COLS)
            mean = mean_buf[row_block(step), columns]
            variance = var_buf[row_block(step), columns]
            damped = clip_factor * mean / (1.0 + variance * inverse)
            new_momentum = beta_outer * own_momentum[row_block(step), columns] + damped
            new_momentum_ref[row_block(step), columns] = new_momentum
            update = outer_rate * (damped + beta_outer * new_momentum)
            old = own_params[row_block(step), columns].astype(jnp.float32)
            new_params_ref[row_block(step), own_columns] = (old - update).astype(jnp.bfloat16)

        for pair in range(1, n_pairs):
            to_pair(step, pair).start()
        to_partner(step, 0).start()

    rms_ref[0] = rms[0, 0]
    mean_var_ref[0] = mean_var[0, 0]
    for step in range(n_steps):
        for pair in range(1, n_pairs):
            from_pair(step, pair).wait()
            to_partner(step, pair).start()
    for step in range(n_steps):
        for hop in range(1, n_rep):
            exchange(step, hop).wait_send()
    pltpu.make_async_copy(others, others, sum_send_sem).wait()
    for step in range(n_steps):
        for pair in range(n_pairs):
            if pair:
                to_pair(step, pair).wait_send()
            to_partner(step, pair).wait_send()
            from_partner(step, pair).wait()


def store(params_ref, momentum_ref, rms_in, mean_var_in, params_out, momentum_out, rms_out, mean_var_out, sem):
    copies = [
        pltpu.make_async_copy(params_ref, params_out, sem.at[0]),
        pltpu.make_async_copy(momentum_ref, momentum_out, sem.at[1]),
    ]
    for copy in copies:
        copy.start()
    rms_out[0] = rms_in[0]
    mean_var_out[0] = mean_var_in[0]
    for copy in copies:
        copy.wait()


def solution(mesh):
    n_rep, n_shard = mesh.shape["rep"], mesh.shape["shard"]

    def shards(delta, counts, params, momentum):
        rows, width = momentum.shape
        full = params.shape[1]
        n_steps = rows // STEP_ROWS
        element_count = rows * width * n_rep * n_shard
        any_space = pl.BlockSpec(memory_space=pl.ANY)
        in_vmem = pl.BlockSpec(memory_space=pltpu.VMEM)
        in_smem = pl.BlockSpec(memory_space=pltpu.SMEM)
        dma = pltpu.SemaphoreType.DMA
        new_params, new_momentum, rms, mean_var = pl.pallas_call(
            functools.partial(kernel, n_rep, n_shard, float(element_count)),
            out_shape=(
                pltpu.VMEM((rows, full), jnp.bfloat16),
                pltpu.VMEM((rows, width), jnp.float32),
                pltpu.SMEM((1,), jnp.float32),
                pltpu.SMEM((1,), jnp.float32),
            ),
            in_specs=[any_space, in_smem, any_space, any_space],
            out_specs=(in_vmem, in_vmem, in_smem, in_smem),
            scratch_shapes=[
                pltpu.VMEM((rows, full), jnp.bfloat16),
                pltpu.VMEM((n_rep - 1, rows, width), jnp.bfloat16),
                pltpu.VMEM((rows, width), jnp.float32),
                pltpu.VMEM((rows, width), jnp.float32),
                pltpu.VMEM((rows, width), jnp.bfloat16),
                pltpu.VMEM((rows, width), jnp.float32),
                pltpu.VMEM((n_rep * n_shard, 2, 128), jnp.float32),
                dma((n_steps,)),
                dma((2,)),
                dma((n_steps, n_rep - 1)),
                dma((n_steps, n_rep - 1)),
                dma,
                dma,
                dma((n_steps, n_rep - 1)),
                dma((n_steps, n_rep - 1)),
                pltpu.SemaphoreType.REGULAR((n_shard.bit_length() + 1,)),
            ],
            compiler_params=pltpu.CompilerParams(collective_id=0, has_side_effects=True),
        )(delta, counts, params, momentum)
        new_params, new_momentum, rms, mean_var = pl.pallas_call(
            store,
            out_shape=(
                jax.ShapeDtypeStruct((rows, full), jnp.bfloat16),
                jax.ShapeDtypeStruct((rows, width), jnp.float32),
                jax.ShapeDtypeStruct((1,), jnp.float32),
                jax.ShapeDtypeStruct((1,), jnp.float32),
            ),
            in_specs=[any_space, any_space, in_smem, in_smem],
            out_specs=(any_space, any_space, in_smem, in_smem),
            scratch_shapes=[dma((2,))],
        )(
            pltpu.with_memory_space_constraint(new_params, pltpu.VMEM),
            pltpu.with_memory_space_constraint(new_momentum, pltpu.VMEM),
            rms,
            mean_var,
        )
        return new_params, new_momentum, rms.reshape(()), mean_var.reshape(())

    return jax.shard_map(
        shards,
        mesh=mesh,
        in_specs=(P("rep", "shard", None), P(), P("shard", None), P("shard", "rep")),
        out_specs=(P("shard", None), P("shard", "rep"), P(), P()),
        check_vma=False,
    )
```

profile of v0, /device:TPU:0, one launch (start us, length us, event | category | flops | bytes accessed | tf_op | source)
XLA Modules:
  0.0 29.9 jit_solution(18359461322668270020)
XLA Ops:
  0.6 27.7 %shard_map.75 = (bf16[64,6144]{1,0:T(8,128)(2,1)S(1)}, f32[64,1536]{1,0:T(8,128)S(1)}, f32[1]{0:T(128)S(4)}, f32[1]{0:T(128)S(4)}) custom-call(bf16[1,64,6144]{2,1,0:T(8,128)(2,1)} %delta_ref.1, s32[4]{0:T(128)} %counts_ref.1, bf16[64,6144]{1,0:T(8,128)(2,1)} %params_ref.1, f32[64,1536]{1,0:T(8,128)} %momentum_ref.1), custom_call_target="tpu_custom_call" | custom-call | tf_op jit(solution)/shard_map/pallas_call | solution.py:277
  28.4 1.6 %shard_map.76 = (bf16[64,6144]{1,0:T(8,128)(2,1)}, f32[64,1536]{1,0:T(8,128)}, f32[1]{0:T(128)}, f32[1]{0:T(128)}) custom-call(bf16[64,6144]{1,0:T(8,128)(2,1)S(1)} %get-tuple-element.12.params_ref, f32[64,1536]{1,0:T(8,128)S(1)} %get-tuple-element.13.momentum_ref, f32[1]{0:T(128)S(4)} %get-tuple-element.14.rms_in, f32[1]{0:T(128)S(4)} %get-tuple-element.15.mean_var_in), custom_call_target="tpu_custom_call" | custom-call | tf_op jit(solution)/shard_map/pallas_call | solution.py:307
where the time goes:
time: 30.1 us; the launch traced here: 29.9 us
  Pallas kernels  29.3 us (97%)
  between operations  0.64 us (2%)
    pallas_call x1, Pallas kernels, shards(): pl.pallas_call(functools.partial(kernel, n_rep, n_shard, float(element_co...  27.7 us
    pallas_call x1, Pallas kernels, shards(): pl.pallas_call(store, out_shape=(jax.ShapeDtypeStruct((rows, full), jnp.b...  1.55 us

commit v1 on v0

--- a/solution.py
+++ b/solution.py
@@ -13,8 +13,8 @@
 epsilon = 1e-06
 
 MESH = pl.DeviceIdType.MESH
-STEP_ROWS = 32
-STEP_COLS = 256
+STEP_ROWS = 16
+STEP_COLS = 512
 UNROLL_MOST = 64
 
 
@@ -22,7 +22,7 @@
     n_rep, n_shard, element_count,
     delta_ref, counts_ref, params_ref, momentum_ref,
     new_params_ref, new_momentum_ref, rms_ref, mean_var_ref,
-    staged, arrived, mean_buf, var_buf, own_params, own_momentum, sums,
+    staged, arrived, mean_buf, var_buf, own_params, own_momentum, sums, tokens,
     stage_sem, local_sem, send_sem, recv_sem, sum_send_sem, sum_recv_sem, out_send_sem, out_recv_sem, round_sem,
 ):
     rep = lax.axis_index("rep")
@@ -48,6 +48,9 @@
         return (other // n_shard, lax.rem(other, n_shard))
 
     barrier = pltpu.get_barrier_semaphore()
+    inner = 2 if n_shard % 2 == 0 else 1
+    n_outer = n_shard // inner
+    outer = shard // inner
 
     def along_shard(offset):
         return (rep, lax.rem(shard + offset, n_shard))
@@ -55,17 +58,34 @@
     def across_rep(hop):
         return (lax.rem(rep + hop, n_rep), shard)
 
-    beside = sorted({1 % n_shard, (n_shard - 1) % n_shard} - {0})
-    greeted = [across_rep(hop) for hop in range(1, n_rep)] + [along_shard(offset) for offset in beside]
-    for device in greeted:
-        pl.semaphore_signal(barrier, inc=1, device_id=device, device_id_type=MESH)
+    def signal_line(semaphore, distance):
+        for at in (outer + distance, outer - distance):
+
+            @pl.when((at >= 0) & (at < n_outer))
+            def _():
+                device = (rep, at * inner + lax.rem(shard, inner))
+                pl.semaphore_signal(semaphore, inc=1, device_id=device, device_id_type=MESH)
+
+    def on_line(distance):
+        return (outer + distance < n_outer).astype(jnp.int32) + (outer >= distance).astype(jnp.int32)
+
+    for hop in range(1, n_rep):
+        pl.semaphore_signal(barrier, inc=1, device_id=across_rep(hop), device_id_type=MESH)
+    if inner == 2:
+        beside = (rep, shard + 1 - 2 * lax.rem(shard, 2))
+        pl.semaphore_signal(barrier, inc=1, device_id=beside, device_id_type=MESH)
+    if n_outer > 1:
+        signal_line(barrier, 1)
 
     for step in range(n_steps):
         stage(step).start()
+    load_counts = pltpu.make_async_copy(counts_ref, tokens, local_sem.at[2])
+    load_counts.start()
     load_params = pltpu.make_async_copy(params_ref.at[:, column_block(rep)], own_params, local_sem.at[0])
     load_momentum = pltpu.make_async_copy(momentum_ref, own_momentum, local_sem.at[1])
 
-    pl.semaphore_wait(barrier, len(greeted))
+    near = n_rep - 1 + inner - 1
+    pl.semaphore_wait(barrier, near + on_line(1) if n_outer > 1 else near)
 
     def exchange(step, hop):
         peer = lax.rem(rep + hop, n_rep)
@@ -88,25 +108,23 @@
 
     known = 1
     level = 0
-    while known < n_shard // 2:
-        for offset in (known, n_shard - known):
-            pl.semaphore_signal(
-                round_sem.at[level], inc=1, device_id=along_shard(offset), device_id_type=MESH
-            )
-        pl.semaphore_wait(round_sem.at[level], 2)
+    while known < n_outer - 1:
+        signal_line(round_sem.at[level], known)
+        pl.semaphore_wait(round_sem.at[level], on_line(known))
         known, level = 2 * known, level + 1
     for hop in range(1, n_rep):
         pl.semaphore_signal(round_sem.at[level], inc=1, device_id=across_rep(hop), device_id_type=MESH)
     pl.semaphore_wait(round_sem.at[level], n_rep - 1)
 
     tile = (8, 128)
-    total = counts_ref[0]
+    load_counts.wait()
+    total = tokens[0]
     for index in range(1, n_rep):
-        total = total + counts_ref[index]
+        total = total + tokens[index]
     total_tokens = jnp.full(tile, total.astype(jnp.float32))
 
     def weight_of(index):
-        return (jnp.full(tile, counts_ref[index].astype(jnp.float32)) / total_tokens)[0:1, 0:1]
+        return (jnp.full(tile, tokens[index].astype(jnp.float32)) / total_tokens)[0:1, 0:1]
 
     weights = [weight_of(lax.rem(rep + n_rep - hop, n_rep)) for hop in range(n_rep)]
 
@@ -145,8 +163,10 @@
 
         square_sum, var_sum = lax.fori_loop(0, width // STEP_COLS, moments, (square_sum, var_sum), unroll=True)
 
-    sums[me, 0:1, :] = jnp.sum(square_sum, axis=0, keepdims=True)
-    sums[me, 1:2, :] = jnp.sum(var_sum, axis=0, keepdims=True)
+    square_row = jnp.sum(square_sum, axis=0, keepdims=True)
+    var_row = jnp.sum(var_sum, axis=0, keepdims=True)
+    first_half = lax.broadcasted_iota(jnp.int32, (1, 128), 1) < 64
+    sums[me] = jnp.where(first_half, square_row + pltpu.roll(square_row, 64, 1), var_row + pltpu.roll(var_row, 64, 1))
 
     def send_sums(device):
         pltpu.make_async_remote_copy(
@@ -175,9 +195,8 @@
     pltpu.make_async_copy(others, others, sum_recv_sem).wait()
 
     totals = jnp.sum(sums[...], axis=0)
-    totals = jnp.sum(totals, axis=1, keepdims=True)
-    rms = jnp.sqrt(totals[0:1] / element_count)
-    mean_var = totals[1:2] / element_count
+    rms = jnp.sqrt(jnp.sum(jnp.where(first_half, totals, 0.0), axis=1, keepdims=True) / element_count)
+    mean_var = jnp.sum(jnp.where(first_half, 0.0, totals), axis=1, keepdims=True) / element_count
     clip_factor = clip_rms / jnp.maximum(rms, clip_rms)
     inverse = 1.0 / (mean_var + epsilon)
 
@@ -253,11 +272,11 @@
     copies = [
         pltpu.make_async_copy(params_ref, params_out, sem.at[0]),
         pltpu.make_async_copy(momentum_ref, momentum_out, sem.at[1]),
+        pltpu.make_async_copy(rms_in, rms_out, sem.at[2]),
+        pltpu.make_async_copy(mean_var_in, mean_var_out, sem.at[3]),
     ]
     for copy in copies:
         copy.start()
-    rms_out[0] = rms_in[0]
-    mean_var_out[0] = mean_var_in[0]
     for copy in copies:
         copy.wait()
 
@@ -282,7 +301,7 @@
                 pltpu.SMEM((1,), jnp.float32),
                 pltpu.SMEM((1,), jnp.float32),
             ),
-            in_specs=[any_space, in_smem, any_space, any_space],
+            in_specs=[any_space] * 4,
             out_specs=(in_vmem, in_vmem, in_smem, in_smem),
             scratch_shapes=[
                 pltpu.VMEM((rows, full), jnp.bfloat16),
@@ -291,9 +310,10 @@
                 pltpu.VMEM((rows, width), jnp.float32),
                 pltpu.VMEM((rows, width), jnp.bfloat16),
                 pltpu.VMEM((rows, width), jnp.float32),
-                pltpu.VMEM((n_rep * n_shard, 2, 128), jnp.float32),
+                pltpu.VMEM((n_rep * n_shard, 1, 128), jnp.float32),
+                pltpu.SMEM((n_rep,), jnp.int32),
                 dma((n_steps,)),
-                dma((2,)),
+                dma((3,)),
                 dma((n_steps, n_rep - 1)),
                 dma((n_steps, n_rep - 1)),
                 dma,
@@ -313,8 +333,8 @@
                 jax.ShapeDtypeStruct((1,), jnp.float32),
             ),
             in_specs=[any_space, any_space, in_smem, in_smem],
-            out_specs=(any_space, any_space, in_smem, in_smem),
-            scratch_shapes=[dma((2,))],
+            out_specs=(any_space,) * 4,
+            scratch_shapes=[dma((4,))],
         )(
             pltpu.with_memory_space_constraint(new_params, pltpu.VMEM),
             pltpu.with_memory_space_constraint(new_momentum, pltpu.VMEM),

time: 30.1 us -> 28.7 us (0.953)
  Pallas kernels: 29.3 us -> 28 us
    pallas_call x1, Pallas kernels: 27.7 us -> 26.9 us  [shards(): pl.pallas_call(functools.partial(kernel, n_rep, n_shard, float(element_co...]
    pallas_call x1, Pallas kernels: 1.55 us -> 1.06 us  [shards(): pl.pallas_call(store, out_shape=(jax.ShapeDtypeStruct((rows, full), jnp.b...]
where the time goes in v1:
time: 28.7 us; the launch traced here: 28.6 us
  Pallas kernels  28 us (98%)
  between operations  0.64 us (2%)
    pallas_call x1, Pallas kernels, shards(): pl.pallas_call(functools.partial(kernel, n_rep, n_shard, float(element_co...  26.9 us
    pallas_call x1, Pallas kernels, shards(): pl.pallas_call(store, out_shape=(jax.ShapeDtypeStruct((rows, full), jnp.b...  1.06 us

profile of v1, /device:TPU:0, one launch (start us, length us, event | category | flops | bytes accessed | tf_op | source)
XLA Modules:
  0.0 28.6 jit_solution(2103146119190425352)
XLA Ops:
  0.6 26.9 %shard_map.75 = (bf16[64,6144]{1,0:T(8,128)(2,1)S(1)}, f32[64,1536]{1,0:T(8,128)S(1)}, f32[1]{0:T(128)S(4)}, f32[1]{0:T(128)S(4)}) custom-call(bf16[1,64,6144]{2,1,0:T(8,128)(2,1)} %delta_ref.1, s32[4]{0:T(128)} %counts_ref.1, bf16[64,6144]{1,0:T(8,128)(2,1)} %params_ref.1, f32[64,1536]{1,0:T(8,128)} %momentum_ref.1), custom_call_target="tpu_custom_call" | custom-call | tf_op jit(solution)/shard_map/pallas_call | solution.py:296
  27.5 1.1 %shard_map.76 = (bf16[64,6144]{1,0:T(8,128)(2,1)}, f32[64,1536]{1,0:T(8,128)}, f32[1]{0:T(128)}, f32[1]{0:T(128)}) custom-call(bf16[64,6144]{1,0:T(8,128)(2,1)S(1)} %get-tuple-element.12.params_ref, f32[64,1536]{1,0:T(8,128)S(1)} %get-tuple-element.13.momentum_ref, f32[1]{0:T(128)S(4)} %get-tuple-element.14.rms_in, f32[1]{0:T(128)S(4)} %get-tuple-element.15.mean_var_in), custom_call_target="tpu_custom_call" | custom-call | tf_op jit(solution)/shard_map/pallas_call | solution.py:327
